TPU v7x, 32 devices: a whole 2x2x4 slice. The times are simulated.
32 devices in a mesh: fluid: 8 (over y, x, core), solid: 4 (over z).
Axes of the slice: x: 2, y: 2, z: 4, core: 2. Of those that a mesh axis runs over, the one named last changes fastest.
Arguments:
- earlier_thermal_state: float32 [256, 128, 128], P('fluid', 'solid'), may hold values from -6 to 6
- thermal_inertia: float32 [256, 128, 128], P('fluid', 'solid'), may hold values from 0.3 to 3
- boundary_energy_current: float32 [64, 16384], P(None, ('fluid', 'solid')), may hold values from -6 to 6
- jacobian_quad_factors: float32 [64, 32768], P(None, ('fluid', 'solid')), may hold values from 0.05 to 0.4
- patch_holder_liquid: int32 [32768, 1], P(('fluid', 'solid')), may hold values from 0 to 7; in each aligned block of 1024 rows (0 to 1023, 1024 to 2047, ...) at most 512 rows name the same one
- patch_slot_number: int32 [32768], P(('fluid', 'solid')), may hold values from 0 to 511
Outputs:
- thermal_state_guess: float32 [256, 128, 128], P('fluid', 'solid')
- equation_misfit: float32 [256, 128, 128], P('fluid', 'solid')
Inputs may be any that keep to these rules, and one draw needn't show every extreme that they name: `patch_holder_liquid`: within the rows of one device, no owner index is named by more than 512 rows; in the rows of some device one owner index is named by exactly 512 rows.
All inputs are finite; a program needn't handle non-finite values.
Results may differ from a plain program's by a relative error of at most 0.00025.
Values sent between devices are 32-bit elements; how exact they have to be, the bound alone decides.
A program may use at most 64 MiB of HBM per device.

v0:
```python
import jax
import jax.numpy as jnp
from jax import lax
from jax.sharding import PartitionSpec as P

ITERS = 3


def extended(shard, sides, width):
    for axis, dim in sides:
        size, length = (lax.axis_size(axis), shard.shape[dim])
        up = [(i, (i + 1) % size) for i in range(size - 1)]
        down = [(j, i) for i, j in up]
        last = lax.slice_in_dim(shard, length - width, length, axis=dim)
        initial = lax.slice_in_dim(shard, 0, width, axis=dim)
        before = lax.ppermute(last, axis, up)
        after = lax.ppermute(initial, axis, down)
        shard = jnp.concatenate([before, shard, after], axis=dim)
    return shard


def matrix_action(field, thermal_inertia):
    padded = extended(field, (("fluid", 0), ("solid", 1)), 1)
    padded = jnp.pad(padded, ((0, 0), (0, 0), (1, 1)))
    beside = padded[2:, 1:-1, 1:-1] + padded[:-2, 1:-1, 1:-1]
    beside = beside + padded[1:-1, 2:, 1:-1] + padded[1:-1, :-2, 1:-1]
    beside = beside + padded[1:-1, 1:-1, 2:] + padded[1:-1, 1:-1, :-2]
    return (6.0 + thermal_inertia) * field - beside


def paired_sums(equation_misfit, precond, image):
    return lax.psum(
        (jnp.sum(equation_misfit * precond), jnp.sum(image * precond)), ("fluid", "solid")
    )


def per_device(
    earlier_thermal_state,
    thermal_inertia,
    boundary_energy_current,
    jacobian_quad_factors,
    patch_holder_liquid,
    patch_slot_number,
):
    owner_index = patch_holder_liquid[:, 0]
    gathered = lax.all_gather(boundary_energy_current, "fluid", axis=1, tiled=True)
    columns = owner_index * boundary_energy_current.shape[1] + patch_slot_number
    picked = jnp.take(gathered, columns, axis=1)
    source = jnp.sum(jacobian_quad_factors * picked, axis=0).reshape(
        earlier_thermal_state.shape[0], earlier_thermal_state.shape[1]
    )
    forcing_entries = thermal_inertia * earlier_thermal_state
    forcing_entries = forcing_entries.at[:, :, -1].add(source)
    diagonal = 6.0 + thermal_inertia
    thermal_state_guess = earlier_thermal_state
    equation_misfit = forcing_entries - matrix_action(thermal_state_guess, thermal_inertia)
    precond = equation_misfit / diagonal
    image = matrix_action(precond, thermal_inertia)
    norm_now, product = paired_sums(equation_misfit, precond, image)
    update_multiplier = norm_now / product
    update_course = precond
    along = image
    for iteration in range(ITERS):
        thermal_state_guess = thermal_state_guess + update_multiplier * update_course
        equation_misfit = equation_misfit - update_multiplier * along
        if iteration + 1 < ITERS:
            precond = equation_misfit / diagonal
            image = matrix_action(precond, thermal_inertia)
            norm_next, product = paired_sums(equation_misfit, precond, image)
            ratio = norm_next / norm_now
            update_multiplier = norm_next / (product - ratio * norm_next / update_multiplier)
            update_course = precond + ratio * update_course
            along = image + ratio * along
            norm_now = norm_next
    return (thermal_state_guess, equation_misfit)


def solution(mesh):
    return jax.shard_map(
        per_device,
        mesh=mesh,
        in_specs=(
            P("fluid", "solid", None),
            P("fluid", "solid", None),
            P(None, ("fluid", "solid")),
            P(None, ("fluid", "solid")),
            P(("fluid", "solid"), None),
            P(("fluid", "solid")),
        ),
        out_specs=(P("fluid", "solid", None), P("fluid", "solid", None)),
        check_vma=False,
    )
```

profile of v0, /device:TPU:0, one launch (start us, length us, event | category | flops | bytes accessed | tf_op | source)
XLA Modules:
  0.0 248.4 jit_solution(11429353709327466096)
XLA Ops:
  7.2 1.7 copy.158
  9.0 0.8 fusion.27
  9.8 1.3 collective-permute-start
  11.0 3.0 %collective-permute-start.1 = (f32[1,32,128]{2,1,0:T(8,128)S(1)}, f32[1,32,128]{2,1,0:T(8,128)S(1)}, u32[]{:S(2)}, u32[]{:S(2)}) collective-permute-start(f32[1,32,128]{2,1,0:T(8,128)S(1)} %get-tuple-element.58), channel_id=1, source_target_pairs={{0,4},{4,8},{8,12},{12,16},{16,20},{20,24},{24,28},{1,5},{5,9},{9,... | collective-permute-start | bytes 49160 | tf_op jit(solution)/shard_map/ppermute | solution.py:16
  14.1 0.7 broadcast_multiply_fusion
  14.8 0.7 broadcast_clamp_fusion
  15.5 1.3 constant_dynamic-update-slice_fusion.1
  16.8 5.0 %collective-permute-start.3 = (f32[34,1,128]{2,1,0:T(1,128)S(1)}, f32[34,1,128]{2,1,0:T(1,128)S(1)}, u32[]{:S(2)}, u32[]{:S(2)}) collective-permute-start(f32[34,1,128]{2,1,0:T(1,128)S(1)} %get-tuple-element.49), channel_id=1, source_target_pairs={{0,1},{1,2},{2,3},{4,5},{5,6},{6,7},{8,9},{9,10},{10,11},{12,13},{... | collective-permute-start | bytes 52232 | tf_op jit(solution)/shard_map/ppermute | solution.py:16
  21.8 1.3 collective-permute-start.2
  23.1 0.2 copy.159
  23.4 4.1 %collective-permute-done.2 = f32[34,1,128]{2,1,0:T(1,128)S(1)} collective-permute-done((f32[34,1,128]{2,1,0:T(1,128)S(1)}, f32[34,1,128]{2,1,0:T(1,128)S(1)}, u32[]{:S(2)}, u32[]{:S(2)}) %collective-permute-start.2) | collective-permute-done | bytes 17440 | tf_op jit(solution)/shard_map/ppermute | solution.py:17
  27.5 1.7 select_maximum_fusion.12
  29.2 11.8 %all-gather.2.cloned.1.call-done = f32[64,4096]{0,1:T(8,128)} async-done(((f32[64,512]{0,1:T(8,128)}), f32[64,4096]{0,1:T(8,128)}) %all-gather.2.cloned.1.call-update) | async-done | bytes 1048592 | tf_op jit(solution)/shard_map/all_gather | solution.py:46
  41.0 4.4 %gather_fusion = f32[1024,64]{1,0:T(8,128)S(1)} fusion(f32[64,4096]{0,1:T(8,128)} %all-gather.2.cloned.1.call-done, s32[1024]{0:T(1024)S(1)} %broadcast_clamp_fusion), kind=kCustom, calls=%fused_computation | custom fusion | bytes 528384 | tf_op jit(solution)/shard_map/jit(_take)/gather | solution.py:48
  45.4 0.4 fusion.18
  45.7 0.3 reshape.54
  46.1 0.2 slice_add_fusion.8
  46.3 3.0 %scatter-add.4 = f32[32,32,128]{2,1,0:T(8,128)S(1)} dynamic-update-slice(f32[32,32,128]{2,1,0:T(8,128)S(1)} %get-tuple-element.60, f32[32,32,1]{2,1,0:T(8,128)S(1)} %slice_add_fusion.8, s32[]{:T(128)} %constant.45.clone.1, s32[]{:T(128)} %constant.45.clone.1, s32[]{:T(128)} %constant.50.clone.1) | dynamic-update-slice | bytes 8196 | tf_op jit(solution)/shard_map/scatter-add | solution.py:53
  49.4 2.2 add_divide_fusion.2
  51.6 2.1 collective-permute-start.5
  53.8 1.3 collective-permute-start.4
  55.1 2.6 %collective-permute-done.4 = f32[1,32,128]{2,1,0:T(8,128)S(1)} collective-permute-done((f32[1,32,128]{2,1,0:T(8,128)S(1)}, f32[1,32,128]{2,1,0:T(8,128)S(1)}, u32[]{:S(2)}, u32[]{:S(2)}) %collective-permute-start.4) | collective-permute-done | bytes 16416 | tf_op jit(solution)/shard_map/ppermute | solution.py:17
  57.7 3.4 %collective-permute-start.7 = (f32[34,1,128]{2,1,0:T(1,128)S(1)}, f32[34,1,128]{2,1,0:T(1,128)S(1)}, u32[]{:S(2)}, u32[]{:S(2)}) collective-permute-start(f32[34,1,128]{2,1,0:T(1,128)S(1)} %get-tuple-element.47), channel_id=1, source_target_pairs={{0,1},{1,2},{2,3},{4,5},{5,6},{6,7},{8,9},{9,10},{10,11},{12,13},{... | collective-permute-start | bytes 52232 | tf_op jit(solution)/shard_map/ppermute | solution.py:16
  61.1 1.3 collective-permute-start.6
  62.6 4.2 %collective-permute-done.6 = f32[34,1,128]{2,1,0:T(1,128)S(1)} collective-permute-done((f32[34,1,128]{2,1,0:T(1,128)S(1)}, f32[34,1,128]{2,1,0:T(1,128)S(1)}, u32[]{:S(2)}, u32[]{:S(2)}) %collective-permute-start.6) | collective-permute-done | bytes 17440 | tf_op jit(solution)/shard_map/ppermute | solution.py:17
  66.8 0.6 select_maximum_fusion.8
  67.4 1.1 multiply_reduce_fusion.4
  68.5 40.9 %all-reduce.6 = (f32[]{:T(128)}, f32[]{:T(128)}) all-reduce(f32[]{:T(128)} %get-tuple-element.27, f32[]{:T(128)} %get-tuple-element.26), channel_id=1, replica_groups=mesh['fluid'=8,'solid'=4] {'fluid','solid'}, use_global_device_ids=true, to_apply=%region_2.3 | all-reduce | flops 2 | bytes 16 | tf_op jit(solution)/shard_map/psum | solution.py:32
  110.8 1.3 collective-permute-start.9
  112.1 1.3 collective-permute-start.8
  113.4 4.3 %collective-permute-done.8 = f32[1,32,128]{2,1,0:T(8,128)S(1)} collective-permute-done((f32[1,32,128]{2,1,0:T(8,128)S(1)}, f32[1,32,128]{2,1,0:T(8,128)S(1)}, u32[]{:S(2)}, u32[]{:S(2)}) %collective-permute-start.8) | collective-permute-done | bytes 16416 | tf_op jit(solution)/shard_map/ppermute | solution.py:17
  117.7 2.3 collective-permute-start.11
  120.1 1.3 collective-permute-start.10
  121.5 4.2 %collective-permute-done.10 = f32[34,1,128]{2,1,0:T(1,128)S(1)} collective-permute-done((f32[34,1,128]{2,1,0:T(1,128)S(1)}, f32[34,1,128]{2,1,0:T(1,128)S(1)}, u32[]{:S(2)}, u32[]{:S(2)}) %collective-permute-start.10) | collective-permute-done | bytes 17440 | tf_op jit(solution)/shard_map/ppermute | solution.py:17
  125.7 0.6 select_maximum_fusion.4
  126.3 2.0 multiply_reduce_fusion.2
  128.3 42.0 %all-reduce.5 = (f32[]{:T(128)}, f32[]{:T(128)}) all-reduce(f32[]{:T(128)} %get-tuple-element.25, f32[]{:T(128)} %get-tuple-element.24), channel_id=1, replica_groups=mesh['fluid'=8,'solid'=4] {'fluid','solid'}, use_global_device_ids=true, to_apply=%region_6.7 | all-reduce | flops 2 | bytes 16 | tf_op jit(solution)/shard_map/psum | solution.py:32
  174.7 1.4 add_divide_fusion
  176.1 1.3 collective-permute-start.13
  177.4 1.3 collective-permute-start.12
  178.7 4.3 %collective-permute-done.12 = f32[1,32,128]{2,1,0:T(8,128)S(1)} collective-permute-done((f32[1,32,128]{2,1,0:T(8,128)S(1)}, f32[1,32,128]{2,1,0:T(8,128)S(1)}, u32[]{:S(2)}, u32[]{:S(2)}) %collective-permute-start.12) | collective-permute-done | bytes 16416 | tf_op jit(solution)/shard_map/ppermute | solution.py:17
  183.1 2.4 collective-permute-start.15
  185.4 1.3 collective-permute-start.14
  186.9 4.2 %collective-permute-done.14 = f32[34,1,128]{2,1,0:T(1,128)S(1)} collective-permute-done((f32[34,1,128]{2,1,0:T(1,128)S(1)}, f32[34,1,128]{2,1,0:T(1,128)S(1)}, u32[]{:S(2)}, u32[]{:S(2)}) %collective-permute-start.14) | collective-permute-done | bytes 17440 | tf_op jit(solution)/shard_map/ppermute | solution.py:17
  191.1 0.6 select_maximum_fusion
  191.7 1.9 multiply_reduce_fusion
  193.6 41.2 %all-reduce.4 = (f32[]{:T(128)}, f32[]{:T(128)}) all-reduce(f32[]{:T(128)} %get-tuple-element.23, f32[]{:T(128)} %get-tuple-element.22), channel_id=1, replica_groups=mesh['fluid'=8,'solid'=4] {'fluid','solid'}, use_global_device_ids=true, to_apply=%region_10.11 | all-reduce | flops 2 | bytes 16 | tf_op jit(solution)/shard_map/psum | solution.py:32
  238.7 2.8 %multiply_subtract_fusion = (f32[32,32,128]{2,1,0:T(8,128)}, f32[32,32,128]{2,1,0:T(8,128)}) fusion(f32[32,32,128]{2,1,0:T(8,128)} %copy-done.2, f32[32,32,128]{2,1,0:T(8,128)} %get-tuple-element.34, f32[]{:T(128)S(6)} %div.37, f32[]{:T(128)S(6)} %div.39, f32[32,32,128]{2,1,0:T(8,128)} %get-tuple-element.37, f32[32,32,128]{2,1,0:T(8,128)S(1)} %get-tuple-element.40, ...), kind=kLoop, calls=%fused_computation.74 | loop fusion | flops 2097152 | bytes 5242900 | tf_op jit(solution)/shard_map/sub | solution.py:65
  (36 shorter events, 0.8 us)
Async XLA Ops:
  7.2 33.8 %all-gather.2.cloned.1.call-start = ((), (), s32[]{:S(2)}) async-start(), calls=%async_computation | async-start | bytes 2359296 | tf_op jit(solution)/shard_map/all_gather | solution.py:46
  8.9 14.2 %copy-start.6 = (s32[1024]{0:T(1024)S(1)}, s32[1024]{0:T(1024)}, u32[]{:S(2)}) copy-start(s32[1024]{0:T(1024)} %param.13) | copy-start | bytes 12292
  9.0 14.2 %copy-start.5 = (f32[64,1024]{1,0:T(8,128)S(1)}, f32[64,1024]{1,0:T(8,128)}, u32[]{:S(2)}) copy-start(f32[64,1024]{1,0:T(8,128)} %param.11) | copy-start | bytes 786436
  9.8 7.0 %collective-permute-start = (f32[1,32,128]{2,1,0:T(8,128)S(1)}, f32[1,32,128]{2,1,0:T(8,128)S(1)}, u32[]{:S(2)}, u32[]{:S(2)}) collective-permute-start(f32[1,32,128]{2,1,0:T(8,128)S(1)} %get-tuple-element.57), channel_id=1, source_target_pairs={{4,0},{8,4},{12,8},{16,12},{20,16},{24,20},{28,24},{5,1},{9,5},{13... | collective-permute-start | bytes 49160 | tf_op jit(solution)/shard_map/ppermute | solution.py:17
  11.0 4.4 %collective-permute-start.1 = (f32[1,32,128]{2,1,0:T(8,128)S(1)}, f32[1,32,128]{2,1,0:T(8,128)S(1)}, u32[]{:S(2)}, u32[]{:S(2)}) collective-permute-start(f32[1,32,128]{2,1,0:T(8,128)S(1)} %get-tuple-element.58), channel_id=1, source_target_pairs={{0,4},{4,8},{8,12},{12,16},{16,20},{20,24},{24,28},{1,5},{5,9},{9,... | collective-permute-start | bytes 49160 | tf_op jit(solution)/shard_map/ppermute | solution.py:16
  16.8 12.4 %copy-start.4 = (f32[34,32,128]{2,1,0:T(8,128)}, f32[34,32,128]{2,1,0:T(8,128)S(1)}, u32[]{:S(2)}) copy-start(f32[34,32,128]{2,1,0:T(8,128)S(1)} %constant_dynamic-update-slice_fusion) | copy-start | bytes 1671172
  16.8 6.5 %collective-permute-start.3 = (f32[34,1,128]{2,1,0:T(1,128)S(1)}, f32[34,1,128]{2,1,0:T(1,128)S(1)}, u32[]{:S(2)}, u32[]{:S(2)}) collective-permute-start(f32[34,1,128]{2,1,0:T(1,128)S(1)} %get-tuple-element.49), channel_id=1, source_target_pairs={{0,1},{1,2},{2,3},{4,5},{5,6},{6,7},{8,9},{9,10},{10,11},{12,13},{... | collective-permute-start | bytes 52232 | tf_op jit(solution)/shard_map/ppermute | solution.py:16
  21.8 5.7 %collective-permute-start.2 = (f32[34,1,128]{2,1,0:T(1,128)S(1)}, f32[34,1,128]{2,1,0:T(1,128)S(1)}, u32[]{:S(2)}, u32[]{:S(2)}) collective-permute-start(f32[34,1,128]{2,1,0:T(1,128)S(1)} %get-tuple-element.50), channel_id=1, source_target_pairs={{1,0},{2,1},{3,2},{5,4},{6,5},{7,6},{9,8},{10,9},{11,10},{13,12},{... | collective-permute-start | bytes 52232 | tf_op jit(solution)/shard_map/ppermute | solution.py:17
  46.1 3.3 %copy-start = (f32[32,32,128]{2,1,0:T(8,128)S(1)}, f32[32,32,128]{2,1,0:T(8,128)}, u32[]{:S(2)}) copy-start(f32[32,32,128]{2,1,0:T(8,128)} %param.9) | copy-start | bytes 1572868
  46.1 3.3 %copy-start.1 = (f32[32,32,128]{2,1,0:T(8,128)S(1)}, f32[32,32,128]{2,1,0:T(8,128)}, u32[]{:S(2)}) copy-start(f32[32,32,128]{2,1,0:T(8,128)} %param.8) | copy-start | bytes 1572868
  51.6 3.5 %collective-permute-start.5 = (f32[1,32,128]{2,1,0:T(8,128)S(1)}, f32[1,32,128]{2,1,0:T(8,128)S(1)}, u32[]{:S(2)}, u32[]{:S(2)}) collective-permute-start(f32[1,32,128]{2,1,0:T(8,128)S(1)} %get-tuple-element.55), channel_id=1, source_target_pairs={{0,4},{4,8},{8,12},{12,16},{16,20},{20,24},{24,28},{1,5},{5,9},{9,... | collective-permute-start | bytes 49160 | tf_op jit(solution)/shard_map/ppermute | solution.py:16
  53.8 3.9 %collective-permute-start.4 = (f32[1,32,128]{2,1,0:T(8,128)S(1)}, f32[1,32,128]{2,1,0:T(8,128)S(1)}, u32[]{:S(2)}, u32[]{:S(2)}) collective-permute-start(f32[1,32,128]{2,1,0:T(8,128)S(1)} %get-tuple-element.56), channel_id=1, source_target_pairs={{4,0},{8,4},{12,8},{16,12},{20,16},{24,20},{28,24},{5,1},{9,5},{13... | collective-permute-start | bytes 49160 | tf_op jit(solution)/shard_map/ppermute | solution.py:17
  57.7 4.8 %collective-permute-start.7 = (f32[34,1,128]{2,1,0:T(1,128)S(1)}, f32[34,1,128]{2,1,0:T(1,128)S(1)}, u32[]{:S(2)}, u32[]{:S(2)}) collective-permute-start(f32[34,1,128]{2,1,0:T(1,128)S(1)} %get-tuple-element.47), channel_id=1, source_target_pairs={{0,1},{1,2},{2,3},{4,5},{5,6},{6,7},{8,9},{9,10},{10,11},{12,13},{... | collective-permute-start | bytes 52232 | tf_op jit(solution)/shard_map/ppermute | solution.py:16
  61.1 5.6 %collective-permute-start.6 = (f32[34,1,128]{2,1,0:T(1,128)S(1)}, f32[34,1,128]{2,1,0:T(1,128)S(1)}, u32[]{:S(2)}, u32[]{:S(2)}) collective-permute-start(f32[34,1,128]{2,1,0:T(1,128)S(1)} %get-tuple-element.48), channel_id=1, source_target_pairs={{1,0},{2,1},{3,2},{5,4},{6,5},{7,6},{9,8},{10,9},{11,10},{13,12},{... | collective-permute-start | bytes 52232 | tf_op jit(solution)/shard_map/ppermute | solution.py:17
  110.8 17.5 %copy-start.3 = (f32[32,32,128]{2,1,0:T(8,128)}, f32[32,32,128]{2,1,0:T(8,128)S(1)}, u32[]{:S(2)}) copy-start(f32[32,32,128]{2,1,0:T(8,128)S(1)} %get-tuple-element.39) | copy-start | bytes 1572868
  110.8 2.6 %collective-permute-start.9 = (f32[1,32,128]{2,1,0:T(8,128)S(1)}, f32[1,32,128]{2,1,0:T(8,128)S(1)}, u32[]{:S(2)}, u32[]{:S(2)}) collective-permute-start(f32[1,32,128]{2,1,0:T(8,128)S(1)} %get-tuple-element.53), channel_id=1, source_target_pairs={{0,4},{4,8},{8,12},{12,16},{16,20},{20,24},{24,28},{1,5},{5,9},{9,... | collective-permute-start | bytes 49160 | tf_op jit(solution)/shard_map/ppermute | solution.py:16
  112.1 5.6 %collective-permute-start.8 = (f32[1,32,128]{2,1,0:T(8,128)S(1)}, f32[1,32,128]{2,1,0:T(8,128)S(1)}, u32[]{:S(2)}, u32[]{:S(2)}) collective-permute-start(f32[1,32,128]{2,1,0:T(8,128)S(1)} %get-tuple-element.54), channel_id=1, source_target_pairs={{4,0},{8,4},{12,8},{16,12},{20,16},{24,20},{28,24},{5,1},{9,5},{13... | collective-permute-start | bytes 49160 | tf_op jit(solution)/shard_map/ppermute | solution.py:17
  117.7 3.8 %collective-permute-start.11 = (f32[34,1,128]{2,1,0:T(1,128)S(1)}, f32[34,1,128]{2,1,0:T(1,128)S(1)}, u32[]{:S(2)}, u32[]{:S(2)}) collective-permute-start(f32[34,1,128]{2,1,0:T(1,128)S(1)} %get-tuple-element.45), channel_id=1, source_target_pairs={{0,1},{1,2},{2,3},{4,5},{5,6},{6,7},{8,9},{9,10},{10,11},{12,13},{... | collective-permute-start | bytes 52232 | tf_op jit(solution)/shard_map/ppermute | solution.py:16
  120.1 5.6 %collective-permute-start.10 = (f32[34,1,128]{2,1,0:T(1,128)S(1)}, f32[34,1,128]{2,1,0:T(1,128)S(1)}, u32[]{:S(2)}, u32[]{:S(2)}) collective-permute-start(f32[34,1,128]{2,1,0:T(1,128)S(1)} %get-tuple-element.46), channel_id=1, source_target_pairs={{1,0},{2,1},{3,2},{5,4},{6,5},{7,6},{9,8},{10,9},{11,10},{13,12},{... | collective-permute-start | bytes 52232 | tf_op jit(solution)/shard_map/ppermute | solution.py:17
  176.1 17.5 %copy-start.2 = (f32[32,32,128]{2,1,0:T(8,128)}, f32[32,32,128]{2,1,0:T(8,128)S(1)}, u32[]{:S(2)}) copy-start(f32[32,32,128]{2,1,0:T(8,128)S(1)} %get-tuple-element.36) | copy-start | bytes 1572868
  176.1 2.6 %collective-permute-start.13 = (f32[1,32,128]{2,1,0:T(8,128)S(1)}, f32[1,32,128]{2,1,0:T(8,128)S(1)}, u32[]{:S(2)}, u32[]{:S(2)}) collective-permute-start(f32[1,32,128]{2,1,0:T(8,128)S(1)} %get-tuple-element.51), channel_id=1, source_target_pairs={{0,4},{4,8},{8,12},{12,16},{16,20},{20,24},{24,28},{1,5},{5,9},{9,... | collective-permute-start | bytes 49160 | tf_op jit(solution)/shard_map/ppermute | solution.py:16
  177.4 5.6 %collective-permute-start.12 = (f32[1,32,128]{2,1,0:T(8,128)S(1)}, f32[1,32,128]{2,1,0:T(8,128)S(1)}, u32[]{:S(2)}, u32[]{:S(2)}) collective-permute-start(f32[1,32,128]{2,1,0:T(8,128)S(1)} %get-tuple-element.52), channel_id=1, source_target_pairs={{4,0},{8,4},{12,8},{16,12},{20,16},{24,20},{28,24},{5,1},{9,5},{13... | collective-permute-start | bytes 49160 | tf_op jit(solution)/shard_map/ppermute | solution.py:17
  183.1 3.8 %collective-permute-start.15 = (f32[34,1,128]{2,1,0:T(1,128)S(1)}, f32[34,1,128]{2,1,0:T(1,128)S(1)}, u32[]{:S(2)}, u32[]{:S(2)}) collective-permute-start(f32[34,1,128]{2,1,0:T(1,128)S(1)} %get-tuple-element.43), channel_id=1, source_target_pairs={{0,1},{1,2},{2,3},{4,5},{5,6},{6,7},{8,9},{9,10},{10,11},{12,13},{... | collective-permute-start | bytes 52232 | tf_op jit(solution)/shard_map/ppermute | solution.py:16
  185.4 5.6 %collective-permute-start.14 = (f32[34,1,128]{2,1,0:T(1,128)S(1)}, f32[34,1,128]{2,1,0:T(1,128)S(1)}, u32[]{:S(2)}, u32[]{:S(2)}) collective-permute-start(f32[34,1,128]{2,1,0:T(1,128)S(1)} %get-tuple-element.44), channel_id=1, source_target_pairs={{1,0},{2,1},{3,2},{5,4},{6,5},{7,6},{9,8},{10,9},{11,10},{13,12},{... | collective-permute-start | bytes 52232 | tf_op jit(solution)/shard_map/ppermute | solution.py:17
Sparse Core Ops, SparseCore 0:
  10.4 30.4 all-gather.1
where the time goes:
time: 250 us; the launch traced here: 248 us
  blocking collectives  124 us (50%)
  waiting for transfers between devices  40.2 us (16%)
  starting transfers between devices  31.2 us (12%)
  between operations  24 us (10%)
  other arithmetic  18.4 us (7%)
  local copies, waits for them, and re-layouts  10.6 us (4%)
    psum x3, blocking collectives, paired_sums(): lax.psum((jnp.sum(equation_misfit * precond), jnp.sum(image * precond)),...  124 us
    ppermute x8, waiting for transfers between devices, extended(): after = lax.ppermute(initial, axis, down)  28 us
    ppermute x8, starting transfers between devices, extended(): before = lax.ppermute(last, axis, up)  20.8 us
    all_gather x1, waiting for transfers between devices, per_device(): lax.all_gather(boundary_energy_current, 'fluid', axis=1, tiled=True)  11.8 us
    ppermute x8, starting transfers between devices, extended(): after = lax.ppermute(initial, axis, down)  10.3 us
  transfers between devices with their start and end apart: 17, of which 11 were waited for; matrix products, arithmetic and copies ran while one was open for 2% of the time, Pallas kernels for 0%

commit v1 on v0

v1 whole, which is shorter than its diff:
```python
import functools

import jax
import jax.numpy as jnp
from jax import lax
from jax.experimental import pallas as pl
from jax.experimental.pallas import tpu as pltpu

ITERS = 3
W = 4
YO = 8
MESH = pl.DeviceIdType.MESH


def kernel(
    nf, ns, t_hbm, i_hbm, face_hbm, jac_hbm, own_hbm, slot_hbm,
    x_hbm, r_hbm,
    t_ext, i_ext, dinv, v0, v1, v2, v3, gath, onehot, jac, own, slot,
    pk_lo, pk_hi, rc_lo, rc_hi, src, src_rc, src_t, sums, xo, ro,
    in_sem, h_send, h_recv, f_send, f_recv, f_relay, s_send, s_recv, a_send, a_recv, out_sem,
):
    n = nf * ns
    cx, cy = t_hbm.shape[0], t_hbm.shape[1]
    f, s = lax.axis_index("fluid"), lax.axis_index("solid")
    me = f * ns + s
    up_f, dn_f = lax.rem(f + 1, nf), lax.rem(f + nf - 1, nf)
    up_s, dn_s = lax.rem(s + 1, ns), lax.rem(s + ns - 1, ns)
    lx = pl.ds(W, cx)
    ly = pl.ds(YO, cy)

    loads = [
        pltpu.make_async_copy(face_hbm, gath.at[f], in_sem.at[0]),
        pltpu.make_async_copy(t_hbm, t_ext.at[lx, ly], in_sem.at[1]),
        pltpu.make_async_copy(i_hbm, i_ext.at[lx, ly], in_sem.at[2]),
        pltpu.make_async_copy(slot_hbm, slot, in_sem.at[3]),
        pltpu.make_async_copy(own_hbm, own, in_sem.at[4]),
        pltpu.make_async_copy(jac_hbm, jac, in_sem.at[5]),
    ]
    for load in loads:
        load.start()

    barrier = pltpu.get_barrier_semaphore()

    def greet(k, _):
        to = lax.rem(me + k, n)
        pl.semaphore_signal(
            barrier, inc=1, device_id={"fluid": to // ns, "solid": lax.rem(to, ns)}, device_id_type=MESH
        )
        return 0

    lax.fori_loop(1, n, greet, 0)

    loads[1].wait()
    loads[2].wait()
    pk_lo[:, 0:W, :] = t_ext[lx, YO:YO + W, :]
    pk_lo[:, W:2 * W, :] = i_ext[lx, YO:YO + W, :]
    pk_hi[:, 0:W, :] = t_ext[lx, YO + cy - W:YO + cy, :]
    pk_hi[:, W:2 * W, :] = i_ext[lx, YO + cy - W:YO + cy, :]
    loads[0].wait()
    pl.semaphore_wait(barrier, n - 1)

    def remote(a, b, send, recv, to_f, to_s):
        return pltpu.make_async_remote_copy(
            src_ref=a, dst_ref=b, send_sem=send, recv_sem=recv,
            device_id={"fluid": to_f, "solid": to_s}, device_id_type=MESH,
        )

    pairs = nf // 2
    side = lax.rem(f, 2)
    mate = f + 1 - 2 * side
    mine = f // 2

    def face_copy(to_f, block, send):
        return remote(gath.at[block], gath.at[block], send, f_recv.at[block], to_f, s)

    def peer(j):
        return 2 * lax.rem(mine + j, pairs) + side

    def back(j):
        return 2 * lax.rem(mine + pairs - j, pairs) + side

    def send_face(j, _):
        to = peer(j)
        face_copy(to, f, f_send.at[to]).start()
        return 0

    lax.fori_loop(1, pairs, send_face, 0)
    face_copy(mate, f, f_send.at[mate]).start()

    hi, lo = pl.ds(W + cx, W), pl.ds(0, W)
    first, last = pl.ds(W, W), pl.ds(cx, W)
    pfirst, plast = pl.ds(0, W), pl.ds(cx - W, W)
    halo = []

    def add(a, b, to_f, to_s):
        k = len(halo)
        halo.append(remote(a, b, h_send.at[k], h_recv.at[k], to_f, to_s))

    add(pk_lo, rc_hi.at[lx], f, dn_s)
    add(pk_hi, rc_lo.at[lx], f, up_s)
    add(t_ext.at[first, ly], t_ext.at[hi, ly], dn_f, s)
    add(t_ext.at[last, ly], t_ext.at[lo, ly], up_f, s)
    add(i_ext.at[first, ly], i_ext.at[hi, ly], dn_f, s)
    add(i_ext.at[last, ly], i_ext.at[lo, ly], up_f, s)
    add(pk_lo.at[pfirst], rc_hi.at[hi], dn_f, dn_s)
    add(pk_lo.at[plast], rc_hi.at[lo], up_f, dn_s)
    add(pk_hi.at[pfirst], rc_lo.at[hi], dn_f, up_s)
    add(pk_hi.at[plast], rc_lo.at[lo], up_f, up_s)
    for copy in halo:
        copy.start()

    loads[3].wait()
    loads[4].wait()
    loads[5].wait()
    faces, rows = onehot.shape
    step = 64

    def make_hot(k, _):
        at = pl.multiple_of(k * step, step)
        ids = lax.broadcasted_iota(jnp.int32, (step, rows), 0) + at
        onehot[pl.ds(at, step), :] = jnp.where(ids == slot[...], 1.0, 0.0).astype(jnp.bfloat16)
        return 0

    lax.fori_loop(0, faces // step, make_hot, 0)

    def pick(block, total):
        g = gath[block]
        high = g.astype(jnp.bfloat16)
        low = (g - high.astype(jnp.float32)).astype(jnp.bfloat16)
        both = jnp.dot(
            jnp.concatenate([high, low], axis=0), onehot[...], preferred_element_type=jnp.float32
        )
        q = g.shape[0]
        part = jnp.sum((both[:q] + both[q:]) * jac[...], axis=0, keepdims=True)
        return jnp.where(own[...] == block, part, total)

    total = pick(f, jnp.zeros((1, rows), jnp.float32))

    for copy in halo:
        copy.wait()

    ext = pl.ds(YO - W, cy + 2 * W)
    lanes = t_ext.shape[2]
    lane = lax.broadcasted_iota(jnp.int32, (1, lanes), 1)

    def beside(ref, x, lo_y, num):
        c = ref[x, pl.ds(lo_y, num), :]
        z = jnp.where(lane == 0, 0.0, pltpu.roll(c, 1, 1))
        z = z + jnp.where(lane == lanes - 1, 0.0, pltpu.roll(c, lanes - 1, 1))
        z = z + (ref[x - 1, pl.ds(lo_y, num), :] + ref[x + 1, pl.ds(lo_y, num), :])
        z = z + (ref[x, pl.ds(lo_y - 1, num), :] + ref[x, pl.ds(lo_y + 1, num), :])
        return c, z

    def inverse(a):
        return 1.0 / (6.0 + a)

    def prep(x, _):
        ok = ((x >= W) | (f > 0)) & ((x < W + cx) | (f < nf - 1))
        ok_lo, ok_hi = ok & (s > 0), ok & (s < ns - 1)
        t_ext[x, ly, :] = jnp.where(ok, t_ext[x, ly, :], 0.0)
        dinv[x, ly, :] = jnp.where(ok, inverse(i_ext[x, ly, :]), 0.0)
        a, b = rc_lo[x], rc_hi[x]
        t_ext[x, YO - W:YO, :] = jnp.where(ok_lo, a[:W], 0.0)
        dinv[x, YO - W:YO, :] = jnp.where(ok_lo, inverse(a[W:]), 0.0)
        t_ext[x, YO + cy:YO + cy + W, :] = jnp.where(ok_hi, b[:W], 0.0)
        dinv[x, YO + cy:YO + cy + W, :] = jnp.where(ok_hi, inverse(b[W:]), 0.0)
        return 0

    lax.fori_loop(0, cx + 2 * W, prep, 0)

    def start_field(x, _):
        c, z = beside(t_ext, x, YO - W, cy + 2 * W)
        v0[x, ext, :] = dinv[x, ext, :] * (z - 6.0 * c)
        return 0

    lax.fori_loop(1, cx + 2 * W - 1, start_field, 0)

    def take(j, total):
        block = back(j)
        face_copy(peer(j), block, f_send.at[peer(j)]).wait_recv()
        face_copy(mate, block, f_relay.at[block]).start()
        return pick(block, total)

    total = lax.fori_loop(1, pairs, take, total)

    def take_mate(j, total):
        block = back(j) + 1 - 2 * side
        face_copy(mate, block, f_send.at[mate]).wait_recv()
        return pick(block, total)

    total = lax.fori_loop(0, pairs, take_mate, total)
    src[...] = total.reshape(src.shape)

    around = [
        (a, b) for a in (-1, 0, 1) for b in (-1, 0, 1) if (a, b) != (0, 0)
    ]
    to_f, to_s = {-1: dn_f, 0: f, 1: up_f}, {-1: dn_s, 0: s, 1: up_s}
    spread = [
        remote(src, src_rc.at[k], s_send.at[k], s_recv.at[k], to_f[-a], to_s[-b])
        for k, (a, b) in enumerate(around)
    ]
    for copy in spread:
        copy.start()

    def turned(tile):
        return jnp.concatenate(
            [tile.T, jnp.zeros((tile.shape[1], lanes - tile.shape[0]), jnp.float32)], axis=1
        )

    src_t[1, 1] = turned(src[...])
    for copy in spread:
        copy.wait_recv()
    for k, (a, b) in enumerate(around):
        src_t[a + 1, b + 1] = turned(src_rc[k])
    per = lanes // cy

    end = lane == lanes - 1

    def add_source(x, _):
        g = x + cx - W
        a = g // cx
        xl = g - a * cx
        col = xl // per
        at = (xl - col * per) * cy

        def column(b, y0, num):
            y = pl.multiple_of(at, cy) + y0
            return jnp.where(end, pltpu.roll(src_t[a, b, pl.ds(y, num), :], lanes - 1 - col, 1), 0.0)

        below, inner, above = column(0, cy - 8, 8), column(1, 0, cy), column(2, 0, 8)
        v0[x, ly, :] = v0[x, ly, :] + dinv[x, ly, :] * inner
        ylo, yhi = pl.ds(YO - W, W), pl.ds(YO + cy, W)
        v0[x, ylo, :] = v0[x, ylo, :] + dinv[x, ylo, :] * below[8 - W:]
        v0[x, yhi, :] = v0[x, yhi, :] + dinv[x, yhi, :] * above[:W]
        return 0

    lax.fori_loop(1, cx + 2 * W - 1, add_source, 0)

    def power(ref, out):
        def one(x, _):
            _, z = beside(ref, x, YO - W, cy + 2 * W)
            out[x, ext, :] = dinv[x, ext, :] * z
            return 0
        return one

    lax.fori_loop(2, cx + 2 * W - 2, power(v0, v1), 0)
    lax.fori_loop(3, cx + 2 * W - 3, power(v1, v2), 0)

    def fold(a):
        return jnp.sum(a.reshape(cy // 8, 8, lanes), axis=0)

    def last_power(x, acc):
        c2, z = beside(v2, x, YO, cy)
        c0, c1 = v0[x, ly, :], v1[x, ly, :]
        d = 6.0 + i_ext[x, ly, :]
        v3[x, ly, :] = dinv[x, ly, :] * z
        d0, d1, d2 = d * c0, d * c1, d * c2
        parts = (c0 * d0, c1 * d0, c1 * d1, c2 * d1, c2 * d2, c2 * z)
        return tuple(a + fold(p) for a, p in zip(acc, parts))

    zero = jnp.zeros((8, lanes), jnp.float32)
    acc = lax.fori_loop(W, W + cx, last_power, (zero,) * 6)
    row = jnp.zeros((1, lanes), jnp.float32)
    for k, a in enumerate(acc):
        whole = jnp.sum(jnp.sum(a, axis=0, keepdims=True), axis=1, keepdims=True)
        row = jnp.where(lane == k, whole, row)
    sums[me] = row

    def sum_copy(k, source):
        to = lax.rem(me + k, n)
        return remote(
            sums.at[source], sums.at[source], a_send.at[k], a_recv.at[source], to // ns, lax.rem(to, ns)
        )

    def send_sum(k, _):
        sum_copy(k, me).start()
        return 0

    lax.fori_loop(1, n, send_sum, 0)

    def await_sum(k, _):
        sum_copy(k, lax.rem(me + k, n)).wait_recv()
        return 0

    lax.fori_loop(1, n, await_sum, 0)
    mean = jnp.sum(sums[...], axis=0)
    mu = [
        jnp.broadcast_to(jnp.sum(jnp.where(lane == k, mean, 0.0), axis=1, keepdims=True), (1, lanes))
        for k in range(6)
    ]

    def inner(a, b):
        out = None
        for i, p in enumerate(a):
            for j, q in enumerate(b):
                term = p * q * mu[i + j]
                out = term if out is None else out + term
        return out

    one = jnp.ones((1, lanes), jnp.float32)
    z, p, c = [one], [one], []
    rz = mu[0]
    for it in range(ITERS):
        w = [p[0]] + [p[i] - p[i - 1] for i in range(1, len(p))] + [-p[-1]]
        alpha = rz / inner(p, w)
        c = [(c[i] if i < len(c) else 0.0) + alpha * p[i] for i in range(len(p))]
        if it + 1 < ITERS:
            z = [(z[i] if i < len(z) else 0.0) - alpha * w[i] for i in range(len(w))]
            new = inner(z, z)
            ratio = new / rz
            p = [z[i] + (ratio * p[i] if i < len(p) else 0.0) for i in range(len(z))]
            rz = new
    e0, e1, e2 = one - c[0], c[0] - c[1], c[1] - c[2]

    chunk = 8
    outs = []
    for base in range(0, cx, chunk):
        def finish(k, _, base=base):
            x = base + k + W
            c0, c1, c2, c3 = v0[x, ly, :], v1[x, ly, :], v2[x, ly, :], v3[x, ly, :]
            xo[base + k] = t_ext[x, ly, :] + (c[0] * c0 + c[1] * c1 + c[2] * c2)
            ro[base + k] = (6.0 + i_ext[x, ly, :]) * (e0 * c0 + e1 * c1 + e2 * c2 + c[2] * c3)
            return 0

        lax.fori_loop(0, chunk, finish, 0)
        part = pl.ds(base, chunk)
        k = base // chunk
        for copy in (
            pltpu.make_async_copy(xo.at[part], x_hbm.at[part], out_sem.at[2 * k]),
            pltpu.make_async_copy(ro.at[part], r_hbm.at[part], out_sem.at[2 * k + 1]),
        ):
            copy.start()
            outs.append(copy)

    for copy in spread:
        copy.wait_send()

    def sent_face(j, _):
        to = peer(j)
        face_copy(to, f, f_send.at[to]).wait_send()
        face_copy(mate, back(j), f_relay.at[back(j)]).wait_send()
        return 0

    lax.fori_loop(1, pairs, sent_face, 0)
    face_copy(mate, f, f_send.at[mate]).wait_send()

    def sent_sum(k, _):
        sum_copy(k, me).wait_send()
        return 0

    lax.fori_loop(1, n, sent_sum, 0)
    for copy in outs:
        copy.wait()


def solution(mesh):
    nf, ns = mesh.shape["fluid"], mesh.shape["solid"]
    n = nf * ns

    def per_device(t, inertia, faces, jac, own, slot):
        cx, cy, cz = t.shape
        q, per = faces.shape
        rows = jac.shape[1]
        own, slot = own.reshape(1, rows), slot.reshape(1, rows)
        f32 = jnp.float32
        ext = pltpu.VMEM((cx + 2 * W, cy + 2 * YO, cz), f32)
        vmem = pltpu.VMEM
        dma = pltpu.SemaphoreType.DMA
        shape = jax.ShapeDtypeStruct(t.shape, f32)
        return tuple(pl.pallas_call(
            functools.partial(kernel, nf, ns),
            out_shape=(shape, shape),
            in_specs=[pl.BlockSpec(memory_space=pl.ANY)] * 6,
            out_specs=(pl.BlockSpec(memory_space=pl.ANY),) * 2,
            scratch_shapes=[ext] * 7 + [
                vmem((nf, q, per), f32),
                vmem((per, rows), jnp.bfloat16),
                vmem((q, rows), f32),
                vmem((1, rows), jnp.int32),
                vmem((1, rows), jnp.int32),
                vmem((cx, 2 * W, cz), f32),
                vmem((cx, 2 * W, cz), f32),
                vmem((cx + 2 * W, 2 * W, cz), f32),
                vmem((cx + 2 * W, 2 * W, cz), f32),
                vmem((rows // cz, cz), f32),
                vmem((8, rows // cz, cz), f32),
                vmem((3, 3, cz, cz), f32),
                vmem((n, 1, cz), f32),
                vmem((cx, cy, cz), f32),
                vmem((cx, cy, cz), f32),
                dma((6,)), dma((10,)), dma((10,)), dma((nf,)), dma((nf,)), dma((nf,)),
                dma((8,)), dma((8,)), dma((n,)), dma((n,)), dma((2 * (cx // 8),)),
            ],
            compiler_params=pltpu.CompilerParams(
                collective_id=0, has_side_effects=True, vmem_limit_bytes=50 * 1024 * 1024
            ),
        )(t, inertia, faces, jac, own, slot))

    P = jax.sharding.PartitionSpec
    both = ("fluid", "solid")
    return jax.shard_map(
        per_device,
        mesh=mesh,
        in_specs=(
            P("fluid", "solid", None),
            P("fluid", "solid", None),
            P(None, both),
            P(None, both),
            P(both, None),
            P(both),
        ),
        out_specs=(P("fluid", "solid", None), P("fluid", "solid", None)),
        check_vma=False,
    )
```

time: 250 us -> 56.4 us (0.23)
  blocking collectives: 124 us -> 0 us
  Pallas kernels: 0 us -> 48.5 us
  waiting for transfers between devices: 40.2 us -> 0 us
  starting transfers between devices: 31.2 us -> 0 us
  between operations: 24 us -> 0.65 us
  other arithmetic: 18.4 us -> 0 us
  local copies, waits for them, and re-layouts: 10.6 us -> 6.89 us
    psum x3 -> x0, blocking collectives: 124 us -> none  [paired_sums(): lax.psum((jnp.sum(equation_misfit * precond), jnp.sum(image * precond)),...]
    pallas_call x0 -> x1, Pallas kernels: none -> 48.5 us  [per_device(): pl.pallas_call(functools.partial(kernel, nf, ns), out_shape=(shape, shape...]
    ppermute x16 -> x0, starting transfers between devices: 31.1 us -> none  [the longest x8 20.8 us: extended(): before = lax.ppermute(last, axis, up)]
    ppermute x16 -> x0, waiting for transfers between devices: 28.4 us -> none  [the longest x8 28 us: extended(): after = lax.ppermute(initial, axis, down)]
    all_gather x1 -> x0, waiting for transfers between devices: 11.8 us -> none  [per_device(): lax.all_gather(boundary_energy_current, 'fluid', axis=1, tiled=True)]
    reduce_sum x4 -> x0, other arithmetic: 5.35 us -> none  [the longest x3 4.98 us: paired_sums(): jnp.sum(image * precond)]
    unnamed x17 -> x14, local copies, waits for them, and re-layouts: 1.97 us -> 6.89 us
    gather x1 -> x0, local copies, waits for them, and re-layouts: 4.39 us -> none  [per_device(): picked = jnp.take(gathered, columns, axis=1)]
  transfers between devices with their start and end apart: 17 -> 0, of which waited for: 11 -> 0; matrix products, arithmetic and copies ran while one was open for 2% -> 0% of each run, Pallas kernels for 0% -> 0%
where the time goes in v1:
time: 56.4 us; the launch traced here: 56.1 us
  Pallas kernels  48.5 us (86%)
  local copies, waits for them, and re-layouts  6.89 us (12%)
  between operations  0.65 us (1%)
    pallas_call x1, Pallas kernels, per_device(): pl.pallas_call(functools.partial(kernel, nf, ns), out_shape=(shape, shape...  48.5 us
    unnamed x14, local copies, waits for them, and re-layouts  6.89 us

profile of v1, /device:TPU:0, one launch (start us, length us, event | category | flops | bytes accessed | tf_op | source)
XLA Modules:
  0.0 56.1 jit_solution(11108337314358040054)
XLA Ops:
  0.6 0.0 copy-start
  0.6 1.0 %copy-done = f32[32,32,128]{2,1,0:T(8,128)S(1)} copy-done((f32[32,32,128]{2,1,0:T(8,128)S(1)}, f32[32,32,128]{2,1,0:T(8,128)}, u32[]{:S(2)}) %copy-start) | copy-done | bytes 524312
  1.7 0.0 copy-start.1
  1.7 1.0 %copy-done.1 = f32[32,32,128]{2,1,0:T(8,128)S(1)} copy-done((f32[32,32,128]{2,1,0:T(8,128)S(1)}, f32[32,32,128]{2,1,0:T(8,128)}, u32[]{:S(2)}) %copy-start.1) | copy-done | bytes 524312
  2.7 0.0 copy-start.2
  2.7 0.9 %copy-done.2 = f32[64,1024]{1,0:T(8,128)S(1)} copy-done((f32[64,1024]{1,0:T(8,128)S(1)}, f32[64,1024]{1,0:T(8,128)}, u32[]{:S(2)}) %copy-start.2) | copy-done | bytes 262168
  3.7 0.0 copy-start.3
  3.7 0.9 %copy-done.3 = f32[64,512]{1,0:T(8,128)S(1)} copy-done((f32[64,512]{1,0:T(8,128)S(1)}, f32[64,512]{1,0:T(8,128)}, u32[]{:S(2)}) %copy-start.3) | copy-done | bytes 131096
  4.6 0.0 copy-start.4
  4.6 0.7 %copy-done.4 = s32[1024,1]{0,1:T(1,128)S(1)} copy-done((s32[1024,1]{0,1:T(1,128)S(1)}, s32[1024,1]{0,1:T(1,128)}, u32[]{:S(2)}) %copy-start.4) | copy-done | bytes 4120
  5.3 0.0 copy-start.5
  5.3 0.7 %copy-done.5 = s32[1024]{0:T(1024)S(1)} copy-done((s32[1024]{0:T(1024)S(1)}, s32[1024]{0:T(1024)}, u32[]{:S(2)}) %copy-start.5) | copy-done | bytes 4120
  5.9 48.5 %shard_map.77 = (f32[32,32,128]{2,1,0:T(8,128)S(1)}, f32[32,32,128]{2,1,0:T(8,128)S(1)}) custom-call(f32[32,32,128]{2,1,0:T(8,128)S(1)} %copy-done, f32[32,32,128]{2,1,0:T(8,128)S(1)} %copy-done.1, f32[64,512]{1,0:T(8,128)S(1)} %copy-done.3, f32[64,1024]{1,0:T(8,128)S(1)} %copy-done.2, s32[1,1024]{1,0:T(1,128)S(1)} %bitcast.2, s32[1,1024]{1,0:T(1,128)S(1)} %bitcast.3), custom_call_target="tpu_custom_call" | custom-call | tf_op jit(solution)/shard_map/pallas_call | solution.py:370
  54.5 0.8 %copy.10 = f32[32,32,128]{2,1,0:T(8,128)} copy(f32[32,32,128]{2,1,0:T(8,128)S(1)} %get-tuple-element.4) | data formatting | bytes 1048576
  55.3 0.8 %copy.11 = f32[32,32,128]{2,1,0:T(8,128)} copy(f32[32,32,128]{2,1,0:T(8,128)S(1)} %get-tuple-element.5) | data formatting | bytes 1048576
Async XLA Ops:
  0.6 1.0 %copy-start = (f32[32,32,128]{2,1,0:T(8,128)S(1)}, f32[32,32,128]{2,1,0:T(8,128)}, u32[]{:S(2)}) copy-start(f32[32,32,128]{2,1,0:T(8,128)} %t_hbm.1) | copy-start | bytes 1572868
  1.7 1.0 %copy-start.1 = (f32[32,32,128]{2,1,0:T(8,128)S(1)}, f32[32,32,128]{2,1,0:T(8,128)}, u32[]{:S(2)}) copy-start(f32[32,32,128]{2,1,0:T(8,128)} %i_hbm.1) | copy-start | bytes 1572868
  2.7 0.9 %copy-start.2 = (f32[64,1024]{1,0:T(8,128)S(1)}, f32[64,1024]{1,0:T(8,128)}, u32[]{:S(2)}) copy-start(f32[64,1024]{1,0:T(8,128)} %jac_hbm.1) | copy-start | bytes 786436
  3.7 0.9 %copy-start.3 = (f32[64,512]{1,0:T(8,128)S(1)}, f32[64,512]{1,0:T(8,128)}, u32[]{:S(2)}) copy-start(f32[64,512]{1,0:T(8,128)} %face_hbm.1) | copy-start | bytes 393220
  4.6 0.7 %copy-start.4 = (s32[1024,1]{0,1:T(1,128)S(1)}, s32[1024,1]{0,1:T(1,128)}, u32[]{:S(2)}) copy-start(s32[1024,1]{0,1:T(1,128)} %param.10) | copy-start | bytes 12292
  5.3 0.7 %copy-start.5 = (s32[1024]{0:T(1024)S(1)}, s32[1024]{0:T(1024)}, u32[]{:S(2)}) copy-start(s32[1024]{0:T(1024)} %param.11) | copy-start | bytes 12292

commit v2 on v1

--- a/solution.py
+++ b/solution.py
@@ -10,6 +10,20 @@
 W = 4
 YO = 8
 MESH = pl.DeviceIdType.MESH
+
+
+def sweep(low, high, body, carry=0, unroll=4):
+    steps = (high - low) // unroll
+
+    def block(i, carry):
+        for j in range(unroll):
+            carry = body(low + i * unroll + j, carry)
+        return carry
+
+    carry = lax.fori_loop(0, steps, block, carry)
+    for x in range(low + steps * unroll, high):
+        carry = body(x, carry)
+    return carry
 
 
 def kernel(
@@ -39,6 +53,7 @@
     for load in loads:
         load.start()
 
+    src_rc[...] = jnp.zeros_like(src_rc)
     barrier = pltpu.get_barrier_semaphore()
 
     def greet(k, _):
@@ -84,30 +99,48 @@
         face_copy(to, f, f_send.at[to]).start()
         return 0
 
-    lax.fori_loop(1, pairs, send_face, 0)
-    face_copy(mate, f, f_send.at[mate]).start()
-
     hi, lo = pl.ds(W + cx, W), pl.ds(0, W)
     first, last = pl.ds(W, W), pl.ds(cx, W)
     pfirst, plast = pl.ds(0, W), pl.ds(cx - W, W)
     halo = []
 
-    def add(a, b, to_f, to_s):
+    to_f, to_s = {-1: dn_f, 0: f, 1: up_f}, {-1: dn_s, 0: s, 1: up_s}
+
+    def there(a, b):
+        x, y = f + a, s + b
+        return (x >= 0) & (x < nf) & (y >= 0) & (y < ns)
+
+    def add(a, b, df, ds):
         k = len(halo)
-        halo.append(remote(a, b, h_send.at[k], h_recv.at[k], to_f, to_s))
-
-    add(pk_lo, rc_hi.at[lx], f, dn_s)
-    add(pk_hi, rc_lo.at[lx], f, up_s)
-    add(t_ext.at[first, ly], t_ext.at[hi, ly], dn_f, s)
-    add(t_ext.at[last, ly], t_ext.at[lo, ly], up_f, s)
-    add(i_ext.at[first, ly], i_ext.at[hi, ly], dn_f, s)
-    add(i_ext.at[last, ly], i_ext.at[lo, ly], up_f, s)
-    add(pk_lo.at[pfirst], rc_hi.at[hi], dn_f, dn_s)
-    add(pk_lo.at[plast], rc_hi.at[lo], up_f, dn_s)
-    add(pk_hi.at[pfirst], rc_lo.at[hi], dn_f, up_s)
-    add(pk_hi.at[plast], rc_lo.at[lo], up_f, up_s)
-    for copy in halo:
+        halo.append((remote(a, b, h_send.at[k], h_recv.at[k], to_f[df], to_s[ds]), df, ds))
+
+    add(t_ext.at[first, ly], t_ext.at[hi, ly], -1, 0)
+    add(t_ext.at[last, ly], t_ext.at[lo, ly], 1, 0)
+    add(i_ext.at[first, ly], i_ext.at[hi, ly], -1, 0)
+    add(i_ext.at[last, ly], i_ext.at[lo, ly], 1, 0)
+    add(pk_lo, rc_hi.at[lx], 0, -1)
+    add(pk_hi, rc_lo.at[lx], 0, 1)
+    add(pk_lo.at[pfirst], rc_hi.at[hi], -1, -1)
+    add(pk_lo.at[plast], rc_hi.at[lo], 1, -1)
+    add(pk_hi.at[pfirst], rc_lo.at[hi], -1, 1)
+    add(pk_hi.at[plast], rc_lo.at[lo], 1, 1)
+
+    def each(copies, act, way):
+        for copy, df, ds in copies:
+            pl.when(there(way * df, way * ds))(functools.partial(act, copy))
+
+    def start(copy):
         copy.start()
+
+    def sent(copy):
+        copy.wait_send()
+
+    def received(copy):
+        copy.wait_recv()
+
+    each(halo, start, 1)
+    lax.fori_loop(1, pairs, send_face, 0)
+    face_copy(mate, f, f_send.at[mate]).start()
 
     loads[3].wait()
     loads[4].wait()
@@ -136,8 +169,8 @@
 
     total = pick(f, jnp.zeros((1, rows), jnp.float32))
 
-    for copy in halo:
-        copy.wait()
+    each(halo, received, -1)
+    each(halo, sent, 1)
 
     ext = pl.ds(YO - W, cy + 2 * W)
     lanes = t_ext.shape[2]
@@ -166,14 +199,14 @@
         dinv[x, YO + cy:YO + cy + W, :] = jnp.where(ok_hi, inverse(b[W:]), 0.0)
         return 0
 
-    lax.fori_loop(0, cx + 2 * W, prep, 0)
+    sweep(0, cx + 2 * W, prep)
 
     def start_field(x, _):
         c, z = beside(t_ext, x, YO - W, cy + 2 * W)
         v0[x, ext, :] = dinv[x, ext, :] * (z - 6.0 * c)
         return 0
 
-    lax.fori_loop(1, cx + 2 * W - 1, start_field, 0)
+    sweep(1, cx + 2 * W - 1, start_field)
 
     def take(j, total):
         block = back(j)
@@ -194,13 +227,11 @@
     around = [
         (a, b) for a in (-1, 0, 1) for b in (-1, 0, 1) if (a, b) != (0, 0)
     ]
-    to_f, to_s = {-1: dn_f, 0: f, 1: up_f}, {-1: dn_s, 0: s, 1: up_s}
     spread = [
-        remote(src, src_rc.at[k], s_send.at[k], s_recv.at[k], to_f[-a], to_s[-b])
+        (remote(src, src_rc.at[k], s_send.at[k], s_recv.at[k], to_f[-a], to_s[-b]), -a, -b)
         for k, (a, b) in enumerate(around)
     ]
-    for copy in spread:
-        copy.start()
+    each(spread, start, 1)
 
     def turned(tile):
         return jnp.concatenate(
@@ -208,8 +239,7 @@
         )
 
     src_t[1, 1] = turned(src[...])
-    for copy in spread:
-        copy.wait_recv()
+    each(spread, received, -1)
     for k, (a, b) in enumerate(around):
         src_t[a + 1, b + 1] = turned(src_rc[k])
     per = lanes // cy
@@ -234,7 +264,7 @@
         v0[x, yhi, :] = v0[x, yhi, :] + dinv[x, yhi, :] * above[:W]
         return 0
 
-    lax.fori_loop(1, cx + 2 * W - 1, add_source, 0)
+    sweep(1, cx + 2 * W - 1, add_source)
 
     def power(ref, out):
         def one(x, _):
@@ -243,8 +273,8 @@
             return 0
         return one
 
-    lax.fori_loop(2, cx + 2 * W - 2, power(v0, v1), 0)
-    lax.fori_loop(3, cx + 2 * W - 3, power(v1, v2), 0)
+    sweep(2, cx + 2 * W - 2, power(v0, v1))
+    sweep(3, cx + 2 * W - 3, power(v1, v2))
 
     def fold(a):
         return jnp.sum(a.reshape(cy // 8, 8, lanes), axis=0)
@@ -259,7 +289,7 @@
         return tuple(a + fold(p) for a, p in zip(acc, parts))
 
     zero = jnp.zeros((8, lanes), jnp.float32)
-    acc = lax.fori_loop(W, W + cx, last_power, (zero,) * 6)
+    acc = sweep(W, W + cx, last_power, (zero,) * 6)
     row = jnp.zeros((1, lanes), jnp.float32)
     for k, a in enumerate(acc):
         whole = jnp.sum(jnp.sum(a, axis=0, keepdims=True), axis=1, keepdims=True)
@@ -322,7 +352,7 @@
             ro[base + k] = (6.0 + i_ext[x, ly, :]) * (e0 * c0 + e1 * c1 + e2 * c2 + c[2] * c3)
             return 0
 
-        lax.fori_loop(0, chunk, finish, 0)
+        sweep(0, chunk, finish)
         part = pl.ds(base, chunk)
         k = base // chunk
         for copy in (
@@ -332,8 +362,7 @@
             copy.start()
             outs.append(copy)
 
-    for copy in spread:
-        copy.wait_send()
+    each(spread, sent, 1)
 
     def sent_face(j, _):
         to = peer(j)
@@ -370,8 +399,8 @@
         return tuple(pl.pallas_call(
             functools.partial(kernel, nf, ns),
             out_shape=(shape, shape),
-            in_specs=[pl.BlockSpec(memory_space=pl.ANY)] * 6,
-            out_specs=(pl.BlockSpec(memory_space=pl.ANY),) * 2,
+            in_specs=[pl.BlockSpec(memory_space=pltpu.HBM)] * 6,
+            out_specs=(pl.BlockSpec(memory_space=pltpu.HBM),) * 2,
             scratch_shapes=[ext] * 7 + [
                 vmem((nf, q, per), f32),
                 vmem((per, rows), jnp.bfloat16),
@@ -392,7 +421,7 @@
                 dma((8,)), dma((8,)), dma((n,)), dma((n,)), dma((2 * (cx // 8),)),
             ],
             compiler_params=pltpu.CompilerParams(
-                collective_id=0, has_side_effects=True, vmem_limit_bytes=50 * 1024 * 1024
+                collective_id=0, has_side_effects=True, vmem_limit_bytes=63 * 1024 * 1024
             ),
         )(t, inertia, faces, jac, own, slot))
 

time: 56.4 us -> 37 us (0.66)
  Pallas kernels: 48.5 us -> 33.5 us
  local copies, waits for them, and re-layouts: 6.89 us -> 2.72 us
    pallas_call x1, Pallas kernels: 48.5 us -> 33.5 us  [per_device(): pl.pallas_call(functools.partial(kernel, nf, ns), out_shape=(shape, shape...]
    unnamed x14 -> x4, local copies, waits for them, and re-layouts: 6.89 us -> 2.72 us
where the time goes in v2:
time: 37 us; the launch traced here: 36.8 us
  Pallas kernels  33.5 us (91%)
  local copies, waits for them, and re-layouts  2.72 us (7%)
  between operations  0.65 us (2%)
    pallas_call x1, Pallas kernels, per_device(): pl.pallas_call(functools.partial(kernel, nf, ns), out_shape=(shape, shape...  33.5 us
    unnamed x4, local copies, waits for them, and re-layouts  2.72 us

profile of v2, /device:TPU:0, one launch (start us, length us, event | category | flops | bytes accessed | tf_op | source)
XLA Modules:
  0.0 36.8 jit_solution(11042766567038615731)
XLA Ops:
  0.6 33.5 %shard_map.77 = (f32[32,32,128]{2,1,0:T(8,128)}, f32[32,32,128]{2,1,0:T(8,128)}) custom-call(f32[32,32,128]{2,1,0:T(8,128)} %t_hbm.1, f32[32,32,128]{2,1,0:T(8,128)} %i_hbm.1, f32[64,512]{1,0:T(8,128)} %face_hbm.1, f32[64,1024]{1,0:T(8,128)} %jac_hbm.1, s32[1,1024]{1,0:T(1,128)} %bitcast.2, s32[1,1024]{1,0:T(1,128)} %bitcast.3), custom_call_target="tpu_custom_call" | custom-call | tf_op jit(solution)/shard_map/pallas_call | solution.py:399
  34.1 0.0 copy-start
  34.1 1.9 %copy.10 = f32[32,32,128]{2,1,0:T(8,128)} copy(f32[32,32,128]{2,1,0:T(8,128)} %get-tuple-element.4) | data formatting | bytes 1048576
  36.0 0.0 copy-done
  36.0 0.8 %copy.11 = f32[32,32,128]{2,1,0:T(8,128)} copy(f32[32,32,128]{2,1,0:T(8,128)S(1)} %copy-done) | data formatting | bytes 1048576
Async XLA Ops:
  34.1 1.9 %copy-start = (f32[32,32,128]{2,1,0:T(8,128)S(1)}, f32[32,32,128]{2,1,0:T(8,128)}, u32[]{:S(2)}) copy-start(f32[32,32,128]{2,1,0:T(8,128)} %get-tuple-element.5) | copy-start | bytes 1572868

commit v3 on v2

--- a/solution.py
+++ b/solution.py
@@ -28,10 +28,10 @@
 
 def kernel(
     nf, ns, t_hbm, i_hbm, face_hbm, jac_hbm, own_hbm, slot_hbm,
-    x_hbm, r_hbm,
+    xo, ro,
     t_ext, i_ext, dinv, v0, v1, v2, v3, gath, onehot, jac, own, slot,
-    pk_lo, pk_hi, rc_lo, rc_hi, src, src_rc, src_t, sums, xo, ro,
-    in_sem, h_send, h_recv, f_send, f_recv, f_relay, s_send, s_recv, a_send, a_recv, out_sem,
+    pk_lo, pk_hi, rc_lo, rc_hi, src, src_rc, src_t, sums,
+    in_sem, h_send, h_recv, f_send, f_recv, f_relay, s_send, s_recv, a_send, a_recv,
 ):
     n = nf * ns
     cx, cy = t_hbm.shape[0], t_hbm.shape[1]
@@ -56,91 +56,117 @@
     src_rc[...] = jnp.zeros_like(src_rc)
     barrier = pltpu.get_barrier_semaphore()
 
-    def greet(k, _):
-        to = lax.rem(me + k, n)
+    turns = [s] + [lax.rem(s + k, ns) for k in range(1, ns)]
+
+    def others(act):
+        def line(k, _):
+            to = lax.rem(f + k, nf)
+            for turn in turns:
+                act(to, turn)
+            return 0
+
+        for turn in turns[1:]:
+            act(f, turn)
+        lax.fori_loop(1, nf, line, 0)
+
+    def greet(a, b):
         pl.semaphore_signal(
-            barrier, inc=1, device_id={"fluid": to // ns, "solid": lax.rem(to, ns)}, device_id_type=MESH
+            barrier, inc=1, device_id={"fluid": a, "solid": b}, device_id_type=MESH
         )
-        return 0
-
-    lax.fori_loop(1, n, greet, 0)
-
+
+    others(greet)
+
+    loads[0].wait()
+    pl.semaphore_wait(barrier, n - 1)
+
+    def remote(a, b, send, recv, to_f, to_s):
+        return pltpu.make_async_remote_copy(
+            src_ref=a, dst_ref=b, send_sem=send, recv_sem=recv,
+            device_id={"fluid": to_f, "solid": to_s}, device_id_type=MESH,
+        )
+
+    pairs = nf // 2
+    side = lax.rem(f, 2)
+    mate = f + 1 - 2 * side
+    mine = f // 2
+
+    def face_copy(to_f, block, send):
+        return remote(gath.at[block], gath.at[block], send, f_recv.at[block], to_f, s)
+
+    tree = pairs == 4
+    if tree:
+        across, along = mine + 1 - 2 * lax.rem(mine, 2), lax.rem(mine + 2, 4)
+        pair_a = across + side * (along - across)
+        pair_b = along + side * (across - along)
+        pair_d = lax.rem(across + 2, 4)
+        near_a, near_b, far = 2 * pair_a + side, 2 * pair_b + side, 2 * pair_d + side
+
+    def peer(j):
+        return 2 * lax.rem(mine + j, pairs) + side
+
+    def back(j):
+        return 2 * lax.rem(mine + pairs - j, pairs) + side
+
+    def send_face(j, _):
+        to = peer(j)
+        face_copy(to, f, f_send.at[to]).start()
+        return 0
+
+    hi, lo = pl.ds(W + cx, W), pl.ds(0, W)
+    first, last = pl.ds(W, W), pl.ds(cx, W)
+    pfirst, plast = pl.ds(0, W), pl.ds(cx - W, W)
+    halo = []
+
+    to_f, to_s = {-1: dn_f, 0: f, 1: up_f}, {-1: dn_s, 0: s, 1: up_s}
+
+    def there(a, b):
+        x, y = f + a, s + b
+        return (x >= 0) & (x < nf) & (y >= 0) & (y < ns)
+
+    def add(a, b, df, ds):
+        k = len(halo)
+        halo.append((remote(a, b, h_send.at[k], h_recv.at[k], to_f[df], to_s[ds]), df, ds))
+
+    add(t_ext.at[first, ly], t_ext.at[hi, ly], -1, 0)
+    add(t_ext.at[last, ly], t_ext.at[lo, ly], 1, 0)
+    add(i_ext.at[pl.ds(W, W - 1), ly], i_ext.at[pl.ds(W + cx, W - 1), ly], -1, 0)
+    add(i_ext.at[pl.ds(cx + 1, W - 1), ly], i_ext.at[pl.ds(1, W - 1), ly], 1, 0)
+    add(pk_lo, rc_hi.at[lx], 0, -1)
+    add(pk_hi, rc_lo.at[lx], 0, 1)
+    add(pk_lo.at[pfirst], rc_hi.at[hi], -1, -1)
+    add(pk_lo.at[plast], rc_hi.at[lo], 1, -1)
+    add(pk_hi.at[pfirst], rc_lo.at[hi], -1, 1)
+    add(pk_hi.at[plast], rc_lo.at[lo], 1, 1)
+
+    def each(copies, act, way):
+        for copy, df, ds in copies:
+            pl.when(there(way * df, way * ds))(functools.partial(act, copy))
+
+    def start(copy):
+        copy.start()
+
+    def sent(copy):
+        copy.wait_send()
+
+    def received(copy):
+        copy.wait_recv()
+
+    if tree:
+        direct = [face_copy(near_a, f, f_send.at[0]), face_copy(near_b, f, f_send.at[1]), face_copy(mate, f, f_send.at[2])]
+        onward = face_copy(near_b, near_a, f_send.at[3])
+        passed = [face_copy(mate, block, f_relay.at[k]) for k, block in enumerate((near_a, near_b, far))]
+        for copy in direct:
+            copy.start()
+    else:
+        lax.fori_loop(1, pairs, send_face, 0)
+        face_copy(mate, f, f_send.at[mate]).start()
     loads[1].wait()
     loads[2].wait()
     pk_lo[:, 0:W, :] = t_ext[lx, YO:YO + W, :]
     pk_lo[:, W:2 * W, :] = i_ext[lx, YO:YO + W, :]
     pk_hi[:, 0:W, :] = t_ext[lx, YO + cy - W:YO + cy, :]
     pk_hi[:, W:2 * W, :] = i_ext[lx, YO + cy - W:YO + cy, :]
-    loads[0].wait()
-    pl.semaphore_wait(barrier, n - 1)
-
-    def remote(a, b, send, recv, to_f, to_s):
-        return pltpu.make_async_remote_copy(
-            src_ref=a, dst_ref=b, send_sem=send, recv_sem=recv,
-            device_id={"fluid": to_f, "solid": to_s}, device_id_type=MESH,
-        )
-
-    pairs = nf // 2
-    side = lax.rem(f, 2)
-    mate = f + 1 - 2 * side
-    mine = f // 2
-
-    def face_copy(to_f, block, send):
-        return remote(gath.at[block], gath.at[block], send, f_recv.at[block], to_f, s)
-
-    def peer(j):
-        return 2 * lax.rem(mine + j, pairs) + side
-
-    def back(j):
-        return 2 * lax.rem(mine + pairs - j, pairs) + side
-
-    def send_face(j, _):
-        to = peer(j)
-        face_copy(to, f, f_send.at[to]).start()
-        return 0
-
-    hi, lo = pl.ds(W + cx, W), pl.ds(0, W)
-    first, last = pl.ds(W, W), pl.ds(cx, W)
-    pfirst, plast = pl.ds(0, W), pl.ds(cx - W, W)
-    halo = []
-
-    to_f, to_s = {-1: dn_f, 0: f, 1: up_f}, {-1: dn_s, 0: s, 1: up_s}
-
-    def there(a, b):
-        x, y = f + a, s + b
-        return (x >= 0) & (x < nf) & (y >= 0) & (y < ns)
-
-    def add(a, b, df, ds):
-        k = len(halo)
-        halo.append((remote(a, b, h_send.at[k], h_recv.at[k], to_f[df], to_s[ds]), df, ds))
-
-    add(t_ext.at[first, ly], t_ext.at[hi, ly], -1, 0)
-    add(t_ext.at[last, ly], t_ext.at[lo, ly], 1, 0)
-    add(i_ext.at[first, ly], i_ext.at[hi, ly], -1, 0)
-    add(i_ext.at[last, ly], i_ext.at[lo, ly], 1, 0)
-    add(pk_lo, rc_hi.at[lx], 0, -1)
-    add(pk_hi, rc_lo.at[lx], 0, 1)
-    add(pk_lo.at[pfirst], rc_hi.at[hi], -1, -1)
-    add(pk_lo.at[plast], rc_hi.at[lo], 1, -1)
-    add(pk_hi.at[pfirst], rc_lo.at[hi], -1, 1)
-    add(pk_hi.at[plast], rc_lo.at[lo], 1, 1)
-
-    def each(copies, act, way):
-        for copy, df, ds in copies:
-            pl.when(there(way * df, way * ds))(functools.partial(act, copy))
-
-    def start(copy):
-        copy.start()
-
-    def sent(copy):
-        copy.wait_send()
-
-    def received(copy):
-        copy.wait_recv()
-
     each(halo, start, 1)
-    lax.fori_loop(1, pairs, send_face, 0)
-    face_copy(mate, f, f_send.at[mate]).start()
 
     loads[3].wait()
     loads[4].wait()
@@ -168,6 +194,16 @@
         return jnp.where(own[...] == block, part, total)
 
     total = pick(f, jnp.zeros((1, rows), jnp.float32))
+    if tree:
+        face_copy(mate, mate, f_send.at[0]).wait_recv()
+        total = pick(mate, total)
+        face_copy(mate, near_a, f_send.at[0]).wait_recv()
+        onward.start()
+        passed[0].start()
+        total = pick(near_a, total)
+        face_copy(mate, near_b, f_send.at[0]).wait_recv()
+        passed[1].start()
+        total = pick(near_b, total)
 
     each(halo, received, -1)
     each(halo, sent, 1)
@@ -199,14 +235,14 @@
         dinv[x, YO + cy:YO + cy + W, :] = jnp.where(ok_hi, inverse(b[W:]), 0.0)
         return 0
 
-    sweep(0, cx + 2 * W, prep)
+    sweep(0, cx + 2 * W, prep, unroll=8)
 
     def start_field(x, _):
         c, z = beside(t_ext, x, YO - W, cy + 2 * W)
         v0[x, ext, :] = dinv[x, ext, :] * (z - 6.0 * c)
         return 0
 
-    sweep(1, cx + 2 * W - 1, start_field)
+    sweep(1, cx + 2 * W - 1, start_field, unroll=10)
 
     def take(j, total):
         block = back(j)
@@ -214,14 +250,30 @@
         face_copy(mate, block, f_relay.at[block]).start()
         return pick(block, total)
 
-    total = lax.fori_loop(1, pairs, take, total)
+    def arrived(block):
+        face_copy(mate, block, f_send.at[0]).wait_recv()
+
+    if not tree:
+        total = lax.fori_loop(1, pairs, take, total)
+    else:
+        arrived(far)
+        passed[2].start()
 
     def take_mate(j, total):
         block = back(j) + 1 - 2 * side
         face_copy(mate, block, f_send.at[mate]).wait_recv()
         return pick(block, total)
 
-    total = lax.fori_loop(0, pairs, take_mate, total)
+    if not tree:
+        total = lax.fori_loop(0, pairs, take_mate, total)
+    else:
+        turn_side = 1 - 2 * side
+        for block in (near_a + turn_side, near_b + turn_side):
+            arrived(block)
+            total = pick(block, total)
+        total = pick(far, total)
+        arrived(far + turn_side)
+        total = pick(far + turn_side, total)
     src[...] = total.reshape(src.shape)
 
     around = [
@@ -239,32 +291,39 @@
         )
 
     src_t[1, 1] = turned(src[...])
-    each(spread, received, -1)
-    for k, (a, b) in enumerate(around):
-        src_t[a + 1, b + 1] = turned(src_rc[k])
     per = lanes // cy
-
     end = lane == lanes - 1
 
-    def add_source(x, _):
+    def place(x):
         g = x + cx - W
         a = g // cx
         xl = g - a * cx
         col = xl // per
-        at = (xl - col * per) * cy
-
-        def column(b, y0, num):
-            y = pl.multiple_of(at, cy) + y0
-            return jnp.where(end, pltpu.roll(src_t[a, b, pl.ds(y, num), :], lanes - 1 - col, 1), 0.0)
-
-        below, inner, above = column(0, cy - 8, 8), column(1, 0, cy), column(2, 0, 8)
-        v0[x, ly, :] = v0[x, ly, :] + dinv[x, ly, :] * inner
+        return a, col, (xl - col * per) * cy
+
+    def column(where, b, y0, num):
+        a, col, at = where
+        y = pl.multiple_of(at, cy) + y0
+        return jnp.where(end, pltpu.roll(src_t[a, b, pl.ds(y, num), :], lanes - 1 - col, 1), 0.0)
+
+    def add_inner(x, _):
+        v0[x, ly, :] = v0[x, ly, :] + dinv[x, ly, :] * column(place(x), 1, 0, cy)
+        return 0
+
+    def add_sides(x, _):
+        where = place(x)
         ylo, yhi = pl.ds(YO - W, W), pl.ds(YO + cy, W)
-        v0[x, ylo, :] = v0[x, ylo, :] + dinv[x, ylo, :] * below[8 - W:]
-        v0[x, yhi, :] = v0[x, yhi, :] + dinv[x, yhi, :] * above[:W]
-        return 0
-
-    sweep(1, cx + 2 * W - 1, add_source)
+        v0[x, ylo, :] = v0[x, ylo, :] + dinv[x, ylo, :] * column(where, 0, cy - 8, 8)[8 - W:]
+        v0[x, yhi, :] = v0[x, yhi, :] + dinv[x, yhi, :] * column(where, 2, 0, 8)[:W]
+        return 0
+
+    sweep(W, W + cx, add_inner, unroll=8)
+    each(spread, received, -1)
+    for k, (a, b) in enumerate(around):
+        src_t[a + 1, b + 1] = turned(src_rc[k])
+    sweep(1, W, add_inner, unroll=3)
+    sweep(W + cx, 2 * W + cx - 1, add_inner, unroll=3)
+    sweep(1, cx + 2 * W - 1, add_sides, unroll=10)
 
     def power(ref, out):
         def one(x, _):
@@ -273,8 +332,8 @@
             return 0
         return one
 
-    sweep(2, cx + 2 * W - 2, power(v0, v1))
-    sweep(3, cx + 2 * W - 3, power(v1, v2))
+    sweep(2, cx + 2 * W - 2, power(v0, v1), unroll=9)
+    sweep(3, cx + 2 * W - 3, power(v1, v2), unroll=9)
 
     def fold(a):
         return jnp.sum(a.reshape(cy // 8, 8, lanes), axis=0)
@@ -289,30 +348,18 @@
         return tuple(a + fold(p) for a, p in zip(acc, parts))
 
     zero = jnp.zeros((8, lanes), jnp.float32)
-    acc = sweep(W, W + cx, last_power, (zero,) * 6)
+    acc = sweep(W, W + cx, last_power, (zero,) * 6, unroll=8)
     row = jnp.zeros((1, lanes), jnp.float32)
     for k, a in enumerate(acc):
         whole = jnp.sum(jnp.sum(a, axis=0, keepdims=True), axis=1, keepdims=True)
         row = jnp.where(lane == k, whole, row)
     sums[me] = row
 
-    def sum_copy(k, source):
-        to = lax.rem(me + k, n)
-        return remote(
-            sums.at[source], sums.at[source], a_send.at[k], a_recv.at[source], to // ns, lax.rem(to, ns)
-        )
-
-    def send_sum(k, _):
-        sum_copy(k, me).start()
-        return 0
-
-    lax.fori_loop(1, n, send_sum, 0)
-
-    def await_sum(k, _):
-        sum_copy(k, lax.rem(me + k, n)).wait_recv()
-        return 0
-
-    lax.fori_loop(1, n, await_sum, 0)
+    def sum_copy(a, b, source):
+        return remote(sums.at[source], sums.at[source], a_send.at[a * ns + b], a_recv.at[source], a, b)
+
+    others(lambda a, b: sum_copy(a, b, me).start())
+    others(lambda a, b: sum_copy(a, b, a * ns + b).wait_recv())
     mean = jnp.sum(sums[...], axis=0)
     mu = [
         jnp.broadcast_to(jnp.sum(jnp.where(lane == k, mean, 0.0), axis=1, keepdims=True), (1, lanes))
@@ -343,7 +390,6 @@
     e0, e1, e2 = one - c[0], c[0] - c[1], c[1] - c[2]
 
     chunk = 8
-    outs = []
     for base in range(0, cx, chunk):
         def finish(k, _, base=base):
             x = base + k + W
@@ -352,16 +398,7 @@
             ro[base + k] = (6.0 + i_ext[x, ly, :]) * (e0 * c0 + e1 * c1 + e2 * c2 + c[2] * c3)
             return 0
 
-        sweep(0, chunk, finish)
-        part = pl.ds(base, chunk)
-        k = base // chunk
-        for copy in (
-            pltpu.make_async_copy(xo.at[part], x_hbm.at[part], out_sem.at[2 * k]),
-            pltpu.make_async_copy(ro.at[part], r_hbm.at[part], out_sem.at[2 * k + 1]),
-        ):
-            copy.start()
-            outs.append(copy)
-
+        sweep(0, chunk, finish, unroll=chunk)
     each(spread, sent, 1)
 
     def sent_face(j, _):
@@ -370,15 +407,24 @@
         face_copy(mate, back(j), f_relay.at[back(j)]).wait_send()
         return 0
 
-    lax.fori_loop(1, pairs, sent_face, 0)
-    face_copy(mate, f, f_send.at[mate]).wait_send()
-
-    def sent_sum(k, _):
-        sum_copy(k, me).wait_send()
-        return 0
-
-    lax.fori_loop(1, n, sent_sum, 0)
-    for copy in outs:
+    if tree:
+        for copy in direct + [onward] + passed:
+            copy.wait_send()
+    else:
+        lax.fori_loop(1, pairs, sent_face, 0)
+        face_copy(mate, f, f_send.at[mate]).wait_send()
+
+    others(lambda a, b: sum_copy(a, b, me).wait_send())
+
+
+def deliver(x, r, x_hbm, r_hbm, sem):
+    copies = [
+        pltpu.make_async_copy(x, x_hbm, sem.at[0]),
+        pltpu.make_async_copy(r, r_hbm, sem.at[1]),
+    ]
+    for copy in copies:
+        copy.start()
+    for copy in copies:
         copy.wait()
 
 
@@ -396,11 +442,11 @@
         vmem = pltpu.VMEM
         dma = pltpu.SemaphoreType.DMA
         shape = jax.ShapeDtypeStruct(t.shape, f32)
-        return tuple(pl.pallas_call(
+        held = pl.pallas_call(
             functools.partial(kernel, nf, ns),
-            out_shape=(shape, shape),
+            out_shape=(pltpu.VMEM(t.shape, f32), pltpu.VMEM(t.shape, f32)),
             in_specs=[pl.BlockSpec(memory_space=pltpu.HBM)] * 6,
-            out_specs=(pl.BlockSpec(memory_space=pltpu.HBM),) * 2,
+            out_specs=(pl.BlockSpec(memory_space=pltpu.VMEM),) * 2,
             scratch_shapes=[ext] * 7 + [
                 vmem((nf, q, per), f32),
                 vmem((per, rows), jnp.bfloat16),
@@ -415,15 +461,20 @@
                 vmem((8, rows // cz, cz), f32),
                 vmem((3, 3, cz, cz), f32),
                 vmem((n, 1, cz), f32),
-                vmem((cx, cy, cz), f32),
-                vmem((cx, cy, cz), f32),
                 dma((6,)), dma((10,)), dma((10,)), dma((nf,)), dma((nf,)), dma((nf,)),
-                dma((8,)), dma((8,)), dma((n,)), dma((n,)), dma((2 * (cx // 8),)),
+                dma((8,)), dma((8,)), dma((n,)), dma((n,)),
             ],
             compiler_params=pltpu.CompilerParams(
-                collective_id=0, has_side_effects=True, vmem_limit_bytes=63 * 1024 * 1024
+                collective_id=0, has_side_effects=True, vmem_limit_bytes=65800000
             ),
-        )(t, inertia, faces, jac, own, slot))
+        )(t, inertia, faces, jac, own, slot)
+        return tuple(pl.pallas_call(
+            deliver,
+            out_shape=(shape, shape),
+            in_specs=[pl.BlockSpec(memory_space=pltpu.VMEM)] * 2,
+            out_specs=(pl.BlockSpec(memory_space=pltpu.HBM),) * 2,
+            scratch_shapes=[dma((2,))],
+        )(*[pltpu.with_memory_space_constraint(a, pltpu.VMEM) for a in held]))
 
     P = jax.sharding.PartitionSpec
     both = ("fluid", "solid")

time: 37 us -> 31 us (0.84)
  Pallas kernels: 33.5 us -> 30.2 us
  local copies, waits for them, and re-layouts: 2.72 us -> 0 us
    pallas_call x1 -> x2, Pallas kernels: 33.5 us -> 30.2 us  [the longest x1 29.2 us: per_device(): pl.pallas_call(functools.partial(kernel, nf, ns), out_shape=(pltpu.VMEM(t...]
    unnamed x4 -> x0, local copies, waits for them, and re-layouts: 2.72 us -> none
where the time goes in v3:
time: 31 us; the launch traced here: 30.8 us
  Pallas kernels  30.2 us (97%)
  between operations  0.64 us (2%)
    pallas_call x1, Pallas kernels, per_device(): pl.pallas_call(functools.partial(kernel, nf, ns), out_shape=(pltpu.VMEM(t...  29.2 us
    pallas_call x1, Pallas kernels, per_device(): pl.pallas_call(deliver, out_shape=(shape, shape), in_specs=[pl.BlockSpec(...  0.99 us

profile of v3, /device:TPU:0, one launch (start us, length us, event | category | flops | bytes accessed | tf_op | source)
XLA Modules:
  0.0 30.8 jit_solution(11874663357672291313)
XLA Ops:
  0.6 29.2 %shard_map.77 = (f32[32,32,128]{2,1,0:T(8,128)S(1)}, f32[32,32,128]{2,1,0:T(8,128)S(1)}) custom-call(f32[32,32,128]{2,1,0:T(8,128)} %t_hbm.1, f32[32,32,128]{2,1,0:T(8,128)} %i_hbm.1, f32[64,512]{1,0:T(8,128)} %face_hbm.1, f32[64,1024]{1,0:T(8,128)} %jac_hbm.1, s32[1,1024]{1,0:T(1,128)} %bitcast.2, s32[1,1024]{1,0:T(1,128)} %bitcast.3), custom_call_target="tpu_custom_call" | custom-call | tf_op jit(solution)/shard_map/pallas_call | solution.py:445
  29.8 1.0 %shard_map.78 = (f32[32,32,128]{2,1,0:T(8,128)}, f32[32,32,128]{2,1,0:T(8,128)}) custom-call(f32[32,32,128]{2,1,0:T(8,128)S(1)} %get-tuple-element.4.x, f32[32,32,128]{2,1,0:T(8,128)S(1)} %get-tuple-element.5.r), custom_call_target="tpu_custom_call" | custom-call | tf_op jit(solution)/shard_map/pallas_call | solution.py:471

commit v4 on v3

--- a/solution.py
+++ b/solution.py
@@ -114,7 +114,8 @@
 
     hi, lo = pl.ds(W + cx, W), pl.ds(0, W)
     first, last = pl.ds(W, W), pl.ds(cx, W)
-    pfirst, plast = pl.ds(0, W), pl.ds(cx - W, W)
+    pfirst, plast = pl.ds(0, W - 1), pl.ds(cx - W + 1, W - 1)
+    chi, clo = pl.ds(W + cx, W - 1), pl.ds(1, W - 1)
     halo = []
 
     to_f, to_s = {-1: dn_f, 0: f, 1: up_f}, {-1: dn_s, 0: s, 1: up_s}
@@ -133,10 +134,10 @@
     add(i_ext.at[pl.ds(cx + 1, W - 1), ly], i_ext.at[pl.ds(1, W - 1), ly], 1, 0)
     add(pk_lo, rc_hi.at[lx], 0, -1)
     add(pk_hi, rc_lo.at[lx], 0, 1)
-    add(pk_lo.at[pfirst], rc_hi.at[hi], -1, -1)
-    add(pk_lo.at[plast], rc_hi.at[lo], 1, -1)
-    add(pk_hi.at[pfirst], rc_lo.at[hi], -1, 1)
-    add(pk_hi.at[plast], rc_lo.at[lo], 1, 1)
+    add(pk_lo.at[pfirst], rc_hi.at[chi], -1, -1)
+    add(pk_lo.at[plast], rc_hi.at[clo], 1, -1)
+    add(pk_hi.at[pfirst], rc_lo.at[chi], -1, 1)
+    add(pk_hi.at[plast], rc_lo.at[clo], 1, 1)
 
     def each(copies, act, way):
         for copy, df, ds in copies:
@@ -182,16 +183,23 @@
 
     lax.fori_loop(0, faces // step, make_hot, 0)
 
-    def pick(block, total):
-        g = gath[block]
-        high = g.astype(jnp.bfloat16)
-        low = (g - high.astype(jnp.float32)).astype(jnp.bfloat16)
-        both = jnp.dot(
-            jnp.concatenate([high, low], axis=0), onehot[...], preferred_element_type=jnp.float32
+    q = jac.shape[0]
+
+    def pick(block, total, *more):
+        blocks = (block,) + more
+        parts = []
+        for one in blocks:
+            g = gath[one]
+            high = g.astype(jnp.bfloat16)
+            parts += [high, (g - high.astype(jnp.float32)).astype(jnp.bfloat16)]
+        found = jnp.dot(
+            jnp.concatenate(parts, axis=0), onehot[...], preferred_element_type=jnp.float32
         )
-        q = g.shape[0]
-        part = jnp.sum((both[:q] + both[q:]) * jac[...], axis=0, keepdims=True)
-        return jnp.where(own[...] == block, part, total)
+        for k, one in enumerate(blocks):
+            both = found[2 * q * k:2 * q * (k + 1)]
+            part = jnp.sum((both[:q] + both[q:]) * jac[...], axis=0, keepdims=True)
+            total = jnp.where(own[...] == one, part, total)
+        return total
 
     total = pick(f, jnp.zeros((1, rows), jnp.float32))
     if tree:
@@ -235,14 +243,14 @@
         dinv[x, YO + cy:YO + cy + W, :] = jnp.where(ok_hi, inverse(b[W:]), 0.0)
         return 0
 
-    sweep(0, cx + 2 * W, prep, unroll=8)
+    sweep(0, cx + 2 * W, prep, unroll=20)
 
     def start_field(x, _):
         c, z = beside(t_ext, x, YO - W, cy + 2 * W)
         v0[x, ext, :] = dinv[x, ext, :] * (z - 6.0 * c)
         return 0
 
-    sweep(1, cx + 2 * W - 1, start_field, unroll=10)
+    sweep(1, cx + 2 * W - 1, start_field, unroll=38)
 
     def take(j, total):
         block = back(j)
@@ -268,9 +276,9 @@
         total = lax.fori_loop(0, pairs, take_mate, total)
     else:
         turn_side = 1 - 2 * side
-        for block in (near_a + turn_side, near_b + turn_side):
-            arrived(block)
-            total = pick(block, total)
+        arrived(near_a + turn_side)
+        arrived(near_b + turn_side)
+        total = pick(near_a + turn_side, total, near_b + turn_side)
         total = pick(far, total)
         arrived(far + turn_side)
         total = pick(far + turn_side, total)
@@ -303,7 +311,7 @@
 
     def column(where, b, y0, num):
         a, col, at = where
-        y = pl.multiple_of(at, cy) + y0
+        y = at + y0 if isinstance(at, int) else pl.multiple_of(at, cy) + y0
         return jnp.where(end, pltpu.roll(src_t[a, b, pl.ds(y, num), :], lanes - 1 - col, 1), 0.0)
 
     def add_inner(x, _):
@@ -317,13 +325,14 @@
         v0[x, yhi, :] = v0[x, yhi, :] + dinv[x, yhi, :] * column(where, 2, 0, 8)[:W]
         return 0
 
-    sweep(W, W + cx, add_inner, unroll=8)
+    sweep(W, W + cx, add_inner, unroll=32)
     each(spread, received, -1)
     for k, (a, b) in enumerate(around):
         src_t[a + 1, b + 1] = turned(src_rc[k])
-    sweep(1, W, add_inner, unroll=3)
-    sweep(W + cx, 2 * W + cx - 1, add_inner, unroll=3)
-    sweep(1, cx + 2 * W - 1, add_sides, unroll=10)
+    for x in range(1, cx + 2 * W - 1):
+        if not W <= x < W + cx:
+            add_inner(x, 0)
+        add_sides(x, 0)
 
     def power(ref, out):
         def one(x, _):
@@ -332,8 +341,8 @@
             return 0
         return one
 
-    sweep(2, cx + 2 * W - 2, power(v0, v1), unroll=9)
-    sweep(3, cx + 2 * W - 3, power(v1, v2), unroll=9)
+    sweep(2, cx + 2 * W - 2, power(v0, v1), unroll=36)
+    sweep(3, cx + 2 * W - 3, power(v1, v2), unroll=34)
 
     def fold(a):
         return jnp.sum(a.reshape(cy // 8, 8, lanes), axis=0)
@@ -348,7 +357,7 @@
         return tuple(a + fold(p) for a, p in zip(acc, parts))
 
     zero = jnp.zeros((8, lanes), jnp.float32)
-    acc = sweep(W, W + cx, last_power, (zero,) * 6, unroll=8)
+    acc = sweep(W, W + cx, last_power, (zero,) * 6, unroll=32)
     row = jnp.zeros((1, lanes), jnp.float32)
     for k, a in enumerate(acc):
         whole = jnp.sum(jnp.sum(a, axis=0, keepdims=True), axis=1, keepdims=True)
@@ -359,6 +368,21 @@
         return remote(sums.at[source], sums.at[source], a_send.at[a * ns + b], a_recv.at[source], a, b)
 
     others(lambda a, b: sum_copy(a, b, me).start())
+    each(spread, sent, 1)
+
+    def sent_face(j, _):
+        to = peer(j)
+        face_copy(to, f, f_send.at[to]).wait_send()
+        face_copy(mate, back(j), f_relay.at[back(j)]).wait_send()
+        return 0
+
+    if tree:
+        for copy in direct + [onward] + passed:
+            copy.wait_send()
+    else:
+        lax.fori_loop(1, pairs, sent_face, 0)
+        face_copy(mate, f, f_send.at[mate]).wait_send()
+
     others(lambda a, b: sum_copy(a, b, a * ns + b).wait_recv())
     mean = jnp.sum(sums[...], axis=0)
     mu = [
@@ -399,21 +423,6 @@
             return 0
 
         sweep(0, chunk, finish, unroll=chunk)
-    each(spread, sent, 1)
-
-    def sent_face(j, _):
-        to = peer(j)
-        face_copy(to, f, f_send.at[to]).wait_send()
-        face_copy(mate, back(j), f_relay.at[back(j)]).wait_send()
-        return 0
-
-    if tree:
-        for copy in direct + [onward] + passed:
-            copy.wait_send()
-    else:
-        lax.fori_loop(1, pairs, sent_face, 0)
-        face_copy(mate, f, f_send.at[mate]).wait_send()
-
     others(lambda a, b: sum_copy(a, b, me).wait_send())
 
 

time: 31 us -> 29.5 us (0.952)
  Pallas kernels: 30.2 us -> 28.7 us
    pallas_call x1, Pallas kernels: 29.2 us -> 27.7 us  [per_device(): pl.pallas_call(functools.partial(kernel, nf, ns), out_shape=(pltpu.VMEM(t...]
where the time goes in v4:
time: 29.5 us; the launch traced here: 29.3 us
  Pallas kernels  28.7 us (97%)
  between operations  0.64 us (2%)
    pallas_call x1, Pallas kernels, per_device(): pl.pallas_call(functools.partial(kernel, nf, ns), out_shape=(pltpu.VMEM(t...  27.7 us
    pallas_call x1, Pallas kernels, per_device(): pl.pallas_call(deliver, out_shape=(shape, shape), in_specs=[pl.BlockSpec(...  0.99 us

profile of v4, /device:TPU:0, one launch (start us, length us, event | category | flops | bytes accessed | tf_op | source)
XLA Modules:
  0.0 29.3 jit_solution(5097334930512604743)
XLA Ops:
  0.6 27.7 %shard_map.77 = (f32[32,32,128]{2,1,0:T(8,128)S(1)}, f32[32,32,128]{2,1,0:T(8,128)S(1)}) custom-call(f32[32,32,128]{2,1,0:T(8,128)} %t_hbm.1, f32[32,32,128]{2,1,0:T(8,128)} %i_hbm.1, f32[64,512]{1,0:T(8,128)} %face_hbm.1, f32[64,1024]{1,0:T(8,128)} %jac_hbm.1, s32[1,1024]{1,0:T(1,128)} %bitcast.2, s32[1,1024]{1,0:T(1,128)} %bitcast.3), custom_call_target="tpu_custom_call" | custom-call | tf_op jit(solution)/shard_map/pallas_call | solution.py:454
  28.4 1.0 %shard_map.78 = (f32[32,32,128]{2,1,0:T(8,128)}, f32[32,32,128]{2,1,0:T(8,128)}) custom-call(f32[32,32,128]{2,1,0:T(8,128)S(1)} %get-tuple-element.4.x, f32[32,32,128]{2,1,0:T(8,128)S(1)} %get-tuple-element.5.r), custom_call_target="tpu_custom_call" | custom-call | tf_op jit(solution)/shard_map/pallas_call | solution.py:480
